TPU v7x, 32 devices: a whole 2x2x4 slice. The times are simulated.
32 devices in a mesh: dp: 8 (over y, x, core), mp: 4 (over z).
Axes of the slice: x: 2, y: 2, z: 4, core: 2. Of those that a mesh axis runs over, the one named last changes fastest.
Arguments:
- feature_ids: int32 [8, 2048, 8], P('dp'), may hold values from 0 to 4095
- tables: bfloat16 [8, 4096, 128], P('dp'), may hold values from -5 to 5
- table_of_feature: int32 [8], replicated, may hold values from 0 to 7, each once
- cross_down: bfloat16 [2, 1024, 512], P(None, 'mp'), may hold values from -0.1875 to 0.1875
- cross_up: bfloat16 [2, 1024, 512], P(None, 'mp'), may hold values from -0.125 to 0.125
- cross_bias: float32 [2, 1024], P(None, 'mp'), may hold values from -3 to 3
- tower_weight: bfloat16 [1024, 2048], P('dp', 'mp'), may hold values from -0.1875 to 0.1875
- tower_bias: float32 [2048], P('mp'), may hold values from -3 to 3
Outputs:
- hidden: bfloat16 [2048, 2048], P('dp', 'mp')
Inputs may be any that keep to these rules, and one draw needn't show every extreme that they name: `feature_ids`: each id indexes a row of its own table. `table_of_feature`: each table serves exactly one feature.
All inputs are finite; a program needn't handle non-finite values.
Results may differ from a plain program's by a relative error of at most 0.015.
Values may be sent and summed in bfloat16 or wider, within the bound.
A program may use at most 64 MiB of HBM per device.

v0:
```python
import jax
import jax.numpy as jnp
from jax import lax
from jax.sharding import PartitionSpec as P


def body(
    feature_ids,
    tables,
    table_of_feature,
    cross_down,
    cross_up,
    cross_bias,
    tower_weight,
    tower_bias,
):
    groups = lax.axis_size("dp")
    members = lax.axis_size("mp")
    member = lax.axis_index("mp")
    table_count, batch_size, hot_count = feature_ids.shape
    row_count = batch_size // (groups * members)
    shaped = feature_ids[0].reshape(groups, members, row_count, hot_count)
    own_ids = lax.dynamic_index_in_dim(shaped, member, 1, keepdims=False).reshape(
        groups * row_count, hot_count
    )
    summed = jnp.zeros((groups * row_count, tables.shape[2]), jnp.float32)
    for hot_index in range(hot_count):
        summed = summed + jnp.take(tables[0], own_ids[:, hot_index], axis=0).astype(jnp.float32)
    columns = [summed.astype(jnp.bfloat16)]
    pooled = jnp.stack(columns, axis=1)
    regrouped = lax.all_to_all(pooled, "dp", split_axis=0, concat_axis=1, tiled=True)
    ordered = jnp.take(regrouped, table_of_feature, axis=1)
    by_width = lax.all_to_all(ordered, "mp", split_axis=1, concat_axis=0, tiled=True)
    group_rows = by_width.shape[0]
    embedded = by_width.reshape(group_rows, -1)
    embedded_wide = embedded.astype(jnp.float32)
    crossed = embedded
    layer_total = cross_down.shape[0]
    for layer_index in range(layer_total):
        partial_value = jnp.dot(
            crossed, cross_down[layer_index], preferred_element_type=jnp.float32
        )
        projected = lax.psum(partial_value.astype(jnp.bfloat16), "mp")
        lifted = lax.dot_general(
            projected,
            cross_up[layer_index],
            (((1,), (1,)), ((), ())),
            preferred_element_type=jnp.float32,
        )
        crossed = (
            embedded_wide * (lifted + cross_bias[layer_index]) + crossed.astype(jnp.float32)
        ).astype(jnp.bfloat16)
    full_rows = lax.all_gather(crossed, "mp", axis=1, tiled=True)
    pre_act = jnp.dot(
        full_rows,
        lax.all_gather(tower_weight, "dp", axis=0, tiled=True),
        preferred_element_type=jnp.float32,
    )
    return jax.nn.relu(pre_act + tower_bias).astype(jnp.bfloat16)


def solution(mesh):
    return jax.shard_map(
        body,
        mesh=mesh,
        in_specs=(
            P("dp", None, None),
            P("dp", None, None),
            P(),
            P(None, "mp", None),
            P(None, "mp", None),
            P(None, "mp"),
            P("dp", "mp"),
            P("mp"),
        ),
        out_specs=P("dp", "mp"),
        check_vma=False,
    )
```

profile of v0, /device:TPU:0, one launch (start us, length us, event | category | flops | bytes accessed | tf_op | source)
XLA Modules:
  0.0 143.6 jit_solution(9518459660529289800)
XLA Ops:
  7.4 1.0 reshape_squeeze.3
  8.8 1.3 gather_fusion.2
  10.2 1.3 gather_fusion.3
  11.5 1.3 gather_fusion.4
  12.9 1.3 gather_fusion.5
  14.2 1.3 gather_fusion.6
  15.6 1.3 gather_fusion.7
  17.0 1.3 gather_fusion.8
  18.3 1.3 gather_fusion.1
  19.7 0.8 fusion.16
  21.0 0.7 reduce.4
  21.7 0.7 reshape.125
  22.3 5.3 %all-to-all-start = ((bf16[8,2,4096]{2,1,0:T(2,128)(2,1)}), bf16[8,2,4096]{2,1,0:T(2,128)(2,1)S(1)}, u32[]{:S(2)}, u32[]{:S(2)}) async-start(bf16[8,2,4096]{2,1,0:T(2,128)(2,1)} %reshape.125), calls=%async_computation | async-start | bytes 262144 | tf_op jit(solution)/shard_map/all_to_all | solution.py:31
  27.8 5.4 %all-to-all-done = bf16[8,2,4096]{2,1,0:T(2,128)(2,1)S(1)} async-done(((bf16[8,2,4096]{2,1,0:T(2,128)(2,1)}), bf16[8,2,4096]{2,1,0:T(2,128)(2,1)S(1)}, u32[]{:S(2)}, u32[]{:S(2)}) %all-to-all-start) | async-done | bytes 131104 | tf_op jit(solution)/shard_map/all_to_all | solution.py:31
  34.0 10.6 %all_to_all.33 = bf16[64,8,128]{2,0,1:T(8,128)(2,1)S(1)} all-to-all(bf16[64,8,128]{2,0,1:T(8,128)(2,1)S(1)} %select_bitcast_fusion), channel_id=1, replica_groups=mesh['dp'=8,'mp'=4] {'mp'}, dimensions={1} | all-to-all | bytes 262144 | tf_op jit(solution)/shard_map/all_to_all | solution.py:33
  44.8 0.9 convolution_convert_fusion.1
  45.8 0.6 copy-done.2
  46.4 32.3 %all-reduce.3.cloned.1.call-done = bf16[256,512]{1,0:T(8,128)(2,1)} async-done(((bf16[256,512]{1,0:T(8,128)(2,1)}), bf16[256,512]{1,0:T(8,128)(2,1)}) %all-reduce.3.cloned.1.call-update) | async-done | bytes 262160 | tf_op jit(solution)/shard_map/psum | solution.py:43
  78.8 1.2 fusion.6
  80.0 0.9 convolution_convert_fusion
  81.5 35.0 %all-reduce.5.cloned.1.call-done = bf16[256,512]{1,0:T(8,128)(2,1)} async-done(((bf16[256,512]{1,0:T(8,128)(2,1)}), bf16[256,512]{1,0:T(8,128)(2,1)}) %all-reduce.5.cloned.1.call-update) | async-done | bytes 262160 | tf_op jit(solution)/shard_map/psum | solution.py:43
  116.6 1.2 fusion.7
  117.8 16.0 %all_gather.6 = bf16[256,1024]{1,0:T(8,128)(2,1)S(1)} all-gather(bf16[256,256]{1,0:T(8,128)(2,1)S(1)} %fusion.7), channel_id=1, replica_groups=mesh['dp'=8,'mp'=4] {'mp'}, dimensions={1}, use_global_device_ids=true | all-gather | bytes 655360 | tf_op jit(solution)/shard_map/all_gather | solution.py:53
  133.8 2.4 %fusion.1 = bf16[256,512]{1,0:T(8,128)(2,1)} fusion(bf16[256,1024]{1,0:T(8,128)(2,1)S(1)} %all_gather.6, bf16[1024,512]{1,0:T(8,128)(2,1)} %all-gather.2.cloned.1.call-done, f32[512]{0:T(512)S(1)} %copy-done.4), kind=kOutput, calls=%fused_computation.11 | convolution fusion | flops 268828672 | bytes 1837056 | tf_op jit(solution)/shard_map/dot_general | solution.py:54
  (51 shorter events, 2.5 us)
Async XLA Ops:
  7.4 1.4 %copy-start = (bf16[1,4096,128]{2,1,0:T(8,128)(2,1)S(1)}, bf16[1,4096,128]{2,1,0:T(8,128)(2,1)}, u32[]{:S(2)}) copy-start(bf16[1,4096,128]{2,1,0:T(8,128)(2,1)} %param.11) | copy-start | bytes 3145732
  22.3 5.4 %copy-start.5 = (s32[8]{0:T(128)S(1)}, s32[8]{0:T(128)}, u32[]{:S(2)}) copy-start(s32[8]{0:T(128)} %param.12) | copy-start | bytes 100
  22.3 10.8 %all-to-all-start = ((bf16[8,2,4096]{2,1,0:T(2,128)(2,1)}), bf16[8,2,4096]{2,1,0:T(2,128)(2,1)S(1)}, u32[]{:S(2)}, u32[]{:S(2)}) async-start(bf16[8,2,4096]{2,1,0:T(2,128)(2,1)} %reshape.125), calls=%async_computation | async-start | bytes 262144 | tf_op jit(solution)/shard_map/all_to_all | solution.py:31
  27.7 51.1 %all-reduce.3.cloned.1.call-start = ((), (), s32[]{:S(2)}) async-start(), calls=%async_computation.2 | async-start | bytes 524288 | tf_op jit(solution)/shard_map/psum | solution.py:43
  33.3 11.5 %copy-start.1 = (bf16[2,256,512]{2,1,0:T(8,128)(2,1)S(1)}, bf16[2,256,512]{2,1,0:T(8,128)(2,1)}, u32[]{:S(2)}) copy-start(bf16[2,256,512]{2,1,0:T(8,128)(2,1)} %param.13) | copy-start | bytes 1572868
  44.8 34.0 %copy-start.3 = (bf16[2,256,512]{2,1,0:T(8,128)(2,1)S(1)}, bf16[2,256,512]{2,1,0:T(8,128)(2,1)}, u32[]{:S(2)}) copy-start(bf16[2,256,512]{2,1,0:T(8,128)(2,1)} %param.14) | copy-start | bytes 1572868
  45.7 0.7 copy-start.2
  45.8 70.8 %all-reduce.5.cloned.1.call-start = ((), (), s32[]{:S(2)}) async-start(), calls=%async_computation.3 | async-start | bytes 524288 | tf_op jit(solution)/shard_map/psum | solution.py:43
  80.9 52.8 %all-gather.2.cloned.1.call-start = ((), (), s32[]{:S(2)}) async-start(), calls=%async_computation.4 | async-start | bytes 1179648 | tf_op jit(solution)/shard_map/all_gather | solution.py:56
  117.8 16.0 %copy-start.4 = (f32[512]{0:T(512)S(1)}, f32[512]{0:T(512)}, u32[]{:S(2)}) copy-start(f32[512]{0:T(512)} %param.17) | copy-start | bytes 6148
Sparse Core Ops, SparseCore 0:
  45.9 32.8 all-reduce.2
  81.1 35.4 all-reduce.4
Sparse Core Ops, SparseCore 1:
  83.3 23.1 all-gather.1
where the time goes:
time: 144 us
  waiting for transfers between devices  73.3 us (51%)
  blocking collectives  26.6 us (18%)
  between operations  15.2 us (11%)
  local copies, waits for them, and re-layouts  14.7 us (10%)
  matrix products  6.66 us (5%)
  starting transfers between devices  5.45 us (4%)
  other arithmetic  1.66 us (1%)
    psum x2, waiting for transfers between devices, body(): projected = lax.psum(partial_value.astype(jnp.bfloat16), 'mp')  67.4 us
    all_gather x1, blocking collectives, body(): full_rows = lax.all_gather(crossed, 'mp', axis=1, tiled=True)  16 us
    gather x8, local copies, waits for them, and re-layouts, body(): jnp.take(tables[0], own_ids[:, hot_index], axis=0).astype(jnp.float32)  10.7 us
    all_to_all x1, blocking collectives, body(): lax.all_to_all(ordered, 'mp', split_axis=1, concat_axis=0, tiled=True)  10.6 us
    all_to_all x1, waiting for transfers between devices, body(): lax.all_to_all(pooled, 'dp', split_axis=0, concat_axis=1, tiled=True)  5.4 us
    all_to_all x1, starting transfers between devices, body(): lax.all_to_all(pooled, 'dp', split_axis=0, concat_axis=1, tiled=True)  5.33 us
  transfers between devices with their start and end apart: 4, of which 3 were waited for; matrix products, arithmetic and copies ran while one was open for 1% of the time, Pallas kernels for 0%

commit v1 on v0

--- a/solution.py
+++ b/solution.py
@@ -1,10 +1,14 @@
+import functools
+
 import jax
 import jax.numpy as jnp
 from jax import lax
+from jax.experimental import pallas as pl
+from jax.experimental.pallas import tpu as pltpu
 from jax.sharding import PartitionSpec as P
 
 
-def body(
+def plain_body(
     feature_ids,
     tables,
     table_of_feature,
@@ -59,6 +63,377 @@
     return jax.nn.relu(pre_act + tower_bias).astype(jnp.bfloat16)
 
 
+MESH = pl.DeviceIdType.MESH
+KERNEL_BYTES = 24 * 1024 * 1024
+
+
+def kernel(
+    groups,
+    members,
+    ids,
+    order,
+    table,
+    down,
+    up,
+    bias,
+    tower,
+    tower_bias,
+    out,
+    table_half,
+    table_wide,
+    sums,
+    outbox,
+    pooled,
+    weights,
+    biases,
+    tower_all,
+    crossed_all,
+    local_sem,
+    z_send,
+    z_recv,
+    plane_send,
+    plane_recv,
+    pair_send,
+    pair_recv,
+    bias_send,
+    bias_recv,
+    tower_send,
+    tower_recv,
+    tower_pair_send,
+    tower_pair_recv,
+    pool_send,
+    pool_recv,
+    cross_send,
+    cross_recv,
+):
+    d = lax.axis_index("dp")
+    m = lax.axis_index("mp")
+    chips = groups // 2
+    q = lax.div(d, 2)
+    c = lax.rem(d, 2)
+    partner = q * 2 + 1 - c
+    layers, block, rank = down.shape
+    hots = ids.shape[0] // (groups * sums.shape[0])
+    rows, embed = sums.shape
+    piece = block // groups
+    depth = tower.shape[0]
+    pieces = 2 * layers
+    sends = []
+
+    def wrap(value, size):
+        return lax.rem(value + size, size)
+
+    def send(src, dst, send_sem, recv_sem, to_d, to_m):
+        copy = pltpu.make_async_remote_copy(
+            src_ref=src,
+            dst_ref=dst,
+            send_sem=send_sem,
+            recv_sem=recv_sem,
+            device_id=(to_d, to_m),
+            device_id_type=MESH,
+        )
+        copy.start()
+        sends.append(copy)
+
+    def arrived(ref, send_sem, recv_sem):
+        pltpu.make_async_remote_copy(
+            src_ref=ref,
+            dst_ref=ref,
+            send_sem=send_sem,
+            recv_sem=recv_sem,
+            device_id=(partner, m),
+            device_id_type=MESH,
+        ).wait_recv()
+
+    def same_core(j):
+        return wrap(q + j, chips) * 2 + c
+
+    def slot(p, member, device):
+        start = pl.multiple_of(member * block + device * piece, piece)
+        return weights.at[p, pl.ds(start, piece), :]
+
+    def tower_slot(device):
+        return tower_all.at[pl.ds(pl.multiple_of(device * depth, depth), depth), :]
+
+    def source(p):
+        return (down, up)[p % 2].at[p // 2]
+
+    table_copy = pltpu.make_async_copy(table.at[0], table_half, local_sem.at[0])
+    table_copy.start()
+    locals_ = []
+    for p in range(pieces):
+        start = pl.multiple_of(m * block, block)
+        copy = pltpu.make_async_copy(
+            source(p), weights.at[p, pl.ds(start, block), :], local_sem.at[1 + p]
+        )
+        copy.start()
+        locals_.append(copy)
+    tower_copy = pltpu.make_async_copy(tower, tower_slot(d), local_sem.at[1 + pieces])
+    tower_copy.start()
+    bias_copy = pltpu.make_async_copy(bias, biases.at[m], local_sem.at[2 + pieces])
+    bias_copy.start()
+
+    barrier = pltpu.get_barrier_semaphore()
+    for k in range(1, members):
+        pl.semaphore_signal(barrier, inc=1, device_id=(d, wrap(m + k, members)), device_id_type=MESH)
+    for i in range(1, groups):
+        pl.semaphore_signal(barrier, inc=1, device_id=(wrap(d + i, groups), m), device_id_type=MESH)
+    pl.semaphore_wait(barrier, members - 1 + groups - 1)
+
+    own = pl.ds(pl.multiple_of(d * piece, piece), piece)
+    for p in range(pieces):
+        for k in range(1, members):
+            send(
+                source(p).at[own, :],
+                slot(p, m, d),
+                z_send.at[p, k],
+                z_recv.at[p, k],
+                d,
+                wrap(m + k, members),
+            )
+    for k in range(1, members):
+        send(bias, biases.at[m], bias_send.at[k], bias_recv.at[k], d, wrap(m + k, members))
+
+    def spread(p):
+        for k in range(1, members):
+            came = wrap(m - k, members)
+            arrived(slot(p, came, d), z_send.at[p, k], z_recv.at[p, k])
+            for j in range(1, chips):
+                send(
+                    slot(p, came, d),
+                    slot(p, came, d),
+                    plane_send.at[p, k, j],
+                    plane_recv.at[p, k, j],
+                    same_core(j),
+                    m,
+                )
+            send(
+                slot(p, came, d),
+                slot(p, came, d),
+                plane_send.at[p, k, 0],
+                plane_recv.at[p, k, 0],
+                partner,
+                m,
+            )
+
+    def relay(p):
+        for k in range(1, members):
+            came = wrap(m - k, members)
+            for j in range(1, chips):
+                here = slot(p, came, same_core(-j))
+                arrived(here, plane_send.at[p, k, j], plane_recv.at[p, k, j])
+                send(here, here, pair_send.at[p, k, j], pair_recv.at[p, k, j], partner, m)
+
+    def complete(p):
+        locals_[p].wait()
+        for k in range(1, members):
+            came = wrap(m - k, members)
+            here = slot(p, came, partner)
+            arrived(here, plane_send.at[p, k, 0], plane_recv.at[p, k, 0])
+            for j in range(1, chips):
+                here = slot(p, came, wrap(q - j, chips) * 2 + 1 - c)
+                arrived(here, pair_send.at[p, k, j], pair_recv.at[p, k, j])
+
+    table_copy.wait()
+    table_wide[...] = table_half[...].astype(jnp.float32)
+    step = 16 if rows % 16 == 0 else 8
+
+    def pool(group):
+        def some(index, carry):
+            base = index * step
+            for r in range(step):
+                total = None
+                for hot in range(hots):
+                    at = ids[(hot * groups + group) * rows + base + r]
+                    row = table_wide[pl.ds(at, 1), :]
+                    total = row if total is None else total + row
+                sums[pl.ds(base + r, 1), :] = total
+            return carry
+
+        lax.fori_loop(0, rows // step, some, 0)
+        return sums[...].astype(jnp.bfloat16)
+
+    turn = 0
+    for i in range(1, groups + 1):
+        if i < groups:
+            group = wrap(d + i, groups)
+            outbox[i] = pool(group)
+            send(outbox.at[i], pooled.at[d], pool_send.at[i], pool_recv.at[i], group, m)
+        else:
+            pooled[d] = pool(d)
+        while turn < pieces and (i >= groups or (turn + 1) * groups <= i * pieces):
+            spread(turn)
+            turn += 1
+    tower_copy.wait()
+    for j in range(1, chips):
+        send(tower, tower_slot(d), tower_send.at[j], tower_recv.at[j], same_core(j), m)
+    send(tower, tower_slot(d), tower_send.at[0], tower_recv.at[0], partner, m)
+
+    relay(0)
+    for i in range(1, groups):
+        arrived(pooled.at[wrap(d - i, groups)], pool_send.at[i], pool_recv.at[i])
+    embedded = jnp.concatenate([pooled[order[f]] for f in range(groups)], axis=1)
+    embedded_wide = embedded.astype(jnp.float32)
+    bias_copy.wait()
+    for k in range(1, members):
+        arrived(biases.at[wrap(m - k, members)], bias_send.at[k], bias_recv.at[k])
+    relay(1)
+    crossed = embedded
+    for layer in range(layers):
+        p = 2 * layer
+        complete(p)
+        projected = jnp.dot(crossed, weights[p], preferred_element_type=jnp.float32)
+        projected = projected.astype(jnp.bfloat16)
+        complete(p + 1)
+        if p + 2 < pieces:
+            relay(p + 2)
+        lifted = lax.dot_general(
+            projected,
+            weights[p + 1],
+            (((1,), (1,)), ((), ())),
+            preferred_element_type=jnp.float32,
+        )
+        row = jnp.concatenate([biases[k, layer : layer + 1, :] for k in range(members)], axis=1)
+        crossed = (embedded_wide * (lifted + row) + crossed.astype(jnp.float32)).astype(
+            jnp.bfloat16
+        )
+        if p + 3 < pieces:
+            relay(p + 3)
+    crossed_all[m] = crossed
+    for k in range(1, members):
+        send(
+            crossed_all.at[m],
+            crossed_all.at[m],
+            cross_send.at[k],
+            cross_recv.at[k],
+            d,
+            wrap(m + k, members),
+        )
+    for j in range(1, chips):
+        here = tower_slot(same_core(-j))
+        arrived(here, tower_send.at[j], tower_recv.at[j])
+        send(here, here, tower_pair_send.at[j], tower_pair_recv.at[j], partner, m)
+    arrived(tower_slot(partner), tower_send.at[0], tower_recv.at[0])
+    for j in range(1, chips):
+        here = tower_slot(wrap(q - j, chips) * 2 + 1 - c)
+        arrived(here, tower_pair_send.at[j], tower_pair_recv.at[j])
+
+    def finish(member):
+        value = jnp.dot(crossed_all[member], tower_all[...], preferred_element_type=jnp.float32)
+        value = jnp.maximum(value + tower_bias[...], 0.0).astype(jnp.bfloat16)
+        out[pl.ds(pl.multiple_of(member * rows, rows), rows), :] = value
+
+    finish(m)
+    for k in range(1, members):
+        came = wrap(m - k, members)
+        arrived(crossed_all.at[came], cross_send.at[k], cross_recv.at[k])
+        finish(came)
+    for copy in sends:
+        copy.wait_send()
+
+
+def fused_body(
+    feature_ids,
+    tables,
+    table_of_feature,
+    cross_down,
+    cross_up,
+    cross_bias,
+    tower_weight,
+    tower_bias,
+):
+    groups = lax.axis_size("dp")
+    members = lax.axis_size("mp")
+    member = lax.axis_index("mp")
+    _, batch_size, hot_count = feature_ids.shape
+    rows = batch_size // (groups * members)
+    _, vocab, embed = tables.shape
+    layers, block, rank = cross_down.shape
+    depth, units = tower_weight.shape
+    width = block * members
+    pieces = 2 * layers
+    chips = groups // 2
+    shaped = feature_ids[0].T.reshape(hot_count, groups, members, rows)
+    own_ids = lax.dynamic_index_in_dim(shaped, member, 2, keepdims=False).reshape(-1)
+    dma = pltpu.SemaphoreType.DMA
+    anywhere = pl.BlockSpec(memory_space=pl.ANY)
+    vmem = pl.BlockSpec(memory_space=pltpu.VMEM)
+    smem = pl.BlockSpec(memory_space=pltpu.SMEM)
+    return pl.pallas_call(
+        functools.partial(kernel, groups, members),
+        out_shape=jax.ShapeDtypeStruct((rows * members, units), jnp.bfloat16),
+        in_specs=[smem, smem, anywhere, anywhere, anywhere, vmem, anywhere, vmem],
+        out_specs=vmem,
+        scratch_shapes=[
+            pltpu.VMEM((vocab, embed), jnp.bfloat16),
+            pltpu.VMEM((vocab, embed), jnp.float32),
+            pltpu.VMEM((rows, embed), jnp.float32),
+            pltpu.VMEM((groups, rows, embed), jnp.bfloat16),
+            pltpu.VMEM((groups, rows, embed), jnp.bfloat16),
+            pltpu.VMEM((pieces, width, rank), jnp.bfloat16),
+            pltpu.VMEM((members, layers, block), jnp.float32),
+            pltpu.VMEM((width, units), jnp.bfloat16),
+            pltpu.VMEM((members, rows, width), jnp.bfloat16),
+            dma((3 + pieces,)),
+            dma((pieces, members)),
+            dma((pieces, members)),
+            dma((pieces, members, chips)),
+            dma((pieces, members, chips)),
+            dma((pieces, members, chips)),
+            dma((pieces, members, chips)),
+            dma((members,)),
+            dma((members,)),
+            dma((chips,)),
+            dma((chips,)),
+            dma((chips,)),
+            dma((chips,)),
+            dma((groups,)),
+            dma((groups,)),
+            dma((members,)),
+            dma((members,)),
+        ],
+        compiler_params=pltpu.CompilerParams(
+            collective_id=0, has_side_effects=True, vmem_limit_bytes=48 * 1024 * 1024
+        ),
+    )(
+        own_ids,
+        table_of_feature,
+        tables,
+        cross_down,
+        cross_up,
+        cross_bias,
+        tower_weight,
+        tower_bias.reshape(1, -1),
+    )
+
+
+def body(
+    feature_ids,
+    tables,
+    table_of_feature,
+    cross_down,
+    cross_up,
+    cross_bias,
+    tower_weight,
+    tower_bias,
+):
+    groups = lax.axis_size("dp")
+    members = lax.axis_size("mp")
+    held = 2 * members * (cross_down.size + cross_up.size) + 2 * groups * tower_weight.size
+    fits = held <= KERNEL_BYTES and groups % 2 == 0 and tables.shape[0] == 1
+    chosen = fused_body if fits else plain_body
+    return chosen(
+        feature_ids,
+        tables,
+        table_of_feature,
+        cross_down,
+        cross_up,
+        cross_bias,
+        tower_weight,
+        tower_bias,
+    )
+
+
 def solution(mesh):
     return jax.shard_map(
         body,

time: 144 us -> 53.4 us (0.37)
  waiting for transfers between devices: 73.3 us -> 0 us
  Pallas kernels: 0 us -> 47 us
  blocking collectives: 26.6 us -> 0 us
  between operations: 15.2 us -> 0.05 us
  local copies, waits for them, and re-layouts: 14.7 us -> 5.79 us
  matrix products: 6.66 us -> 0 us
  starting transfers between devices: 5.45 us -> 0 us
  other arithmetic: 1.66 us -> 0 us
    psum x2 -> x0, waiting for transfers between devices: 67.4 us -> none  [body(): projected = lax.psum(partial_value.astype(jnp.bfloat16), 'mp')]
    pallas_call x0 -> x1, Pallas kernels: none -> 47 us  [fused_body(): pl.pallas_call(functools.partial(kernel, groups, members), out_shape=jax....]
    all_gather x1 -> x0, blocking collectives: 16 us -> none  [body(): full_rows = lax.all_gather(crossed, 'mp', axis=1, tiled=True)]
    gather x9 -> x0, local copies, waits for them, and re-layouts: 11.3 us -> none  [the longest x8 10.7 us: body(): jnp.take(tables[0], own_ids[:, hot_index], axis=0).astype(jnp.float32)]
    all_to_all x1 -> x0, blocking collectives: 10.6 us -> none  [body(): lax.all_to_all(ordered, 'mp', split_axis=1, concat_axis=0, tiled=True)]
    dot_general x5 -> x0, matrix products: 6.66 us -> none  [the longest x2 2.42 us: body(): lax.dot_general(projected, cross_up[layer_index], (((1,), (1,)), ((), ())...]
    all_to_all x1 -> x0, waiting for transfers between devices: 5.4 us -> none  [body(): lax.all_to_all(pooled, 'dp', split_axis=0, concat_axis=1, tiled=True)]
    all_to_all x1 -> x0, starting transfers between devices: 5.33 us -> none  [body(): lax.all_to_all(pooled, 'dp', split_axis=0, concat_axis=1, tiled=True)]
  transfers between devices with their start and end apart: 4 -> 0, of which waited for: 3 -> 0; matrix products, arithmetic and copies ran while one was open for 1% -> 0% of each run, Pallas kernels for 0% -> 0%
where the time goes in v1:
time: 53.4 us; the launch traced here: 52.9 us
  Pallas kernels  47 us (88%)
  local copies, waits for them, and re-layouts  5.79 us (11%)
    pallas_call x1, Pallas kernels, fused_body(): pl.pallas_call(functools.partial(kernel, groups, members), out_shape=jax....  47 us
    unnamed x15, local copies, waits for them, and re-layouts  4.62 us

profile of v1, /device:TPU:0, one launch (start us, length us, event | category | flops | bytes accessed | tf_op | source)
XLA Modules:
  0.0 52.9 jit_solution(15928393503183088519)
XLA Ops:
  0.0 0.0 copy-start.3
  0.0 1.0 %reshape.10 = s32[8,8,4,64]{3,2,1,0:T(4,128)S(1)} reshape(s32[8,2048]{1,0:T(8,128)} %bitcast.5) | data formatting | bytes 131072 | tf_op jit(solution)/shard_map/reshape | solution.py:356
  1.0 0.1 dynamic-slice_reduce_fusion
  1.1 0.0 copy-start.4
  1.1 0.0 copy-start.5
  1.1 0.0 copy-start.6
  1.1 0.1 reshape.11.ids
  1.2 0.0 copy-done.3
  1.2 0.6 %copy-done.4 = f32[2,256]{1,0:T(2,128)S(1)} copy-done((f32[2,256]{1,0:T(2,128)S(1)}, f32[2,256]{1,0:T(2,128)}, u32[]{:S(2)}) %copy-start.4) | copy-done | bytes 2072
  1.8 0.0 copy-done.5
  1.8 0.0 copy-done.6
  1.8 0.0 copy-start
  1.8 1.2 %copy-done = bf16[1,4096,128]{2,1,0:T(8,128)(2,1)S(1)} copy-done((bf16[1,4096,128]{2,1,0:T(8,128)(2,1)S(1)}, bf16[1,4096,128]{2,1,0:T(8,128)(2,1)}, u32[]{:S(2)}) %copy-start) | copy-done | bytes 1048600
  3.0 0.0 copy-start.1
  3.0 1.0 %copy-done.1 = bf16[2,256,512]{2,1,0:T(8,128)(2,1)S(1)} copy-done((bf16[2,256,512]{2,1,0:T(8,128)(2,1)S(1)}, bf16[2,256,512]{2,1,0:T(8,128)(2,1)}, u32[]{:S(2)}) %copy-start.1) | copy-done | bytes 524312
  4.1 0.0 copy-start.2
  4.1 1.0 %copy-done.2 = bf16[2,256,512]{2,1,0:T(8,128)(2,1)S(1)} copy-done((bf16[2,256,512]{2,1,0:T(8,128)(2,1)S(1)}, bf16[2,256,512]{2,1,0:T(8,128)(2,1)}, u32[]{:S(2)}) %copy-start.2) | copy-done | bytes 524312
  5.1 47.0 %shard_map.82 = bf16[256,512]{1,0:T(8,128)(2,1)S(1)} custom-call(s32[4096]{0:T(1024)S(1)} %reshape.11.ids, s32[8]{0:T(128)S(1)} %copy-done.6, bf16[1,4096,128]{2,1,0:T(8,128)(2,1)S(1)} %copy-done, bf16[2,256,512]{2,1,0:T(8,128)(2,1)S(1)} %copy-done.1, bf16[2,256,512]{2,1,0:T(8,128)(2,1)S(1)} %copy-done.2, f32[2,256]{1,0:T(2,128)S(1)} %copy-done.4, ...), custom_call_target="tpu_custom_call" | custom-call | tf_op jit(solution)/shard_map/pallas_call | solution.py:362
  52.1 0.7 %copy.10 = bf16[256,512]{1,0:T(8,128)(2,1)} copy(bf16[256,512]{1,0:T(8,128)(2,1)S(1)} %shard_map.82) | data formatting | bytes 524288
Async XLA Ops:
  0.0 1.2 %copy-start.3 = (bf16[128,512]{1,0:T(8,128)(2,1)S(1)}, bf16[128,512]{1,0:T(8,128)(2,1)}, u32[]{:S(2)}) copy-start(bf16[128,512]{1,0:T(8,128)(2,1)} %tower.1) | copy-start | bytes 393220
  1.1 0.7 %copy-start.4 = (f32[2,256]{1,0:T(2,128)S(1)}, f32[2,256]{1,0:T(2,128)}, u32[]{:S(2)}) copy-start(f32[2,256]{1,0:T(2,128)} %bias.1) | copy-start | bytes 6148
  1.1 0.7 %copy-start.5 = (f32[512]{0:T(512)S(1)}, f32[512]{0:T(512)}, u32[]{:S(2)}) copy-start(f32[512]{0:T(512)} %param.15) | copy-start | bytes 6148
  1.1 0.7 %copy-start.6 = (s32[8]{0:T(128)S(1)}, s32[8]{0:T(128)}, u32[]{:S(2)}) copy-start(s32[8]{0:T(128)} %order.1) | copy-start | bytes 100
  1.8 1.2 %copy-start = (bf16[1,4096,128]{2,1,0:T(8,128)(2,1)S(1)}, bf16[1,4096,128]{2,1,0:T(8,128)(2,1)}, u32[]{:S(2)}) copy-start(bf16[1,4096,128]{2,1,0:T(8,128)(2,1)} %table.1) | copy-start | bytes 3145732
  3.0 1.0 %copy-start.1 = (bf16[2,256,512]{2,1,0:T(8,128)(2,1)S(1)}, bf16[2,256,512]{2,1,0:T(8,128)(2,1)}, u32[]{:S(2)}) copy-start(bf16[2,256,512]{2,1,0:T(8,128)(2,1)} %down.1) | copy-start | bytes 1572868
  4.1 1.0 %copy-start.2 = (bf16[2,256,512]{2,1,0:T(8,128)(2,1)S(1)}, bf16[2,256,512]{2,1,0:T(8,128)(2,1)}, u32[]{:S(2)}) copy-start(bf16[2,256,512]{2,1,0:T(8,128)(2,1)} %up.1) | copy-start | bytes 1572868

commit v2 on v1

v2 whole, which is shorter than its diff:
```python
import functools

import jax
import jax.numpy as jnp
from jax import lax
from jax.experimental import pallas as pl
from jax.experimental.pallas import tpu as pltpu
from jax.sharding import PartitionSpec as P


def plain_body(
    feature_ids,
    tables,
    table_of_feature,
    cross_down,
    cross_up,
    cross_bias,
    tower_weight,
    tower_bias,
):
    groups = lax.axis_size("dp")
    members = lax.axis_size("mp")
    member = lax.axis_index("mp")
    table_count, batch_size, hot_count = feature_ids.shape
    row_count = batch_size // (groups * members)
    shaped = feature_ids[0].reshape(groups, members, row_count, hot_count)
    own_ids = lax.dynamic_index_in_dim(shaped, member, 1, keepdims=False).reshape(
        groups * row_count, hot_count
    )
    summed = jnp.zeros((groups * row_count, tables.shape[2]), jnp.float32)
    for hot_index in range(hot_count):
        summed = summed + jnp.take(tables[0], own_ids[:, hot_index], axis=0).astype(jnp.float32)
    columns = [summed.astype(jnp.bfloat16)]
    pooled = jnp.stack(columns, axis=1)
    regrouped = lax.all_to_all(pooled, "dp", split_axis=0, concat_axis=1, tiled=True)
    ordered = jnp.take(regrouped, table_of_feature, axis=1)
    by_width = lax.all_to_all(ordered, "mp", split_axis=1, concat_axis=0, tiled=True)
    group_rows = by_width.shape[0]
    embedded = by_width.reshape(group_rows, -1)
    embedded_wide = embedded.astype(jnp.float32)
    crossed = embedded
    layer_total = cross_down.shape[0]
    for layer_index in range(layer_total):
        partial_value = jnp.dot(
            crossed, cross_down[layer_index], preferred_element_type=jnp.float32
        )
        projected = lax.psum(partial_value.astype(jnp.bfloat16), "mp")
        lifted = lax.dot_general(
            projected,
            cross_up[layer_index],
            (((1,), (1,)), ((), ())),
            preferred_element_type=jnp.float32,
        )
        crossed = (
            embedded_wide * (lifted + cross_bias[layer_index]) + crossed.astype(jnp.float32)
        ).astype(jnp.bfloat16)
    full_rows = lax.all_gather(crossed, "mp", axis=1, tiled=True)
    pre_act = jnp.dot(
        full_rows,
        lax.all_gather(tower_weight, "dp", axis=0, tiled=True),
        preferred_element_type=jnp.float32,
    )
    return jax.nn.relu(pre_act + tower_bias).astype(jnp.bfloat16)


MESH = pl.DeviceIdType.MESH
KERNEL_BYTES = 24 * 1024 * 1024
VMEM_BYTES = (64 * 1024 - 352) * 1024
CHIPS = 4


def kernel(
    groups,
    members,
    ids_hbm,
    order_hbm,
    table,
    down,
    up,
    bias,
    tower,
    tower_bias_hbm,
    out,
    ids,
    order,
    table_half,
    table_wide,
    sums,
    outbox,
    pooled,
    embedded,
    crossed,
    weights,
    biases,
    tower_all,
    tower_bias,
    crossed_all,
    local_sem,
    z_send,
    z_recv,
    plane_send,
    plane_recv,
    diag_send,
    diag_recv,
    pair_send,
    pair_recv,
    bias_send,
    bias_recv,
    t_plane_send,
    t_plane_recv,
    t_diag_send,
    t_diag_recv,
    t_pair_send,
    t_pair_recv,
    pool_send,
    pool_recv,
    cross_send,
    cross_recv,
):
    d = lax.axis_index("dp")
    m = lax.axis_index("mp")
    q = lax.div(d, 2)
    c = lax.rem(d, 2)
    partner = q * 2 + 1 - c
    chip_x = q + 1 - 2 * lax.rem(q, 2)
    chip_y = lax.rem(q + 2, CHIPS)
    chip_z = lax.rem(chip_x + 2, CHIPS)
    chips = (chip_x, chip_y, chip_z)
    layers, block, rank = down.shape
    hots = ids.shape[0]
    rows, embed = sums.shape
    piece = block // groups
    depth = tower.shape[0]
    pieces = 2 * layers
    sends = []
    locals_ = []

    def wrap(value, size):
        return lax.rem(value + size, size)

    def load(src, dst):
        copy = pltpu.make_async_copy(src, dst, local_sem.at[len(locals_)])
        copy.start()
        locals_.append(copy)
        return copy

    def send(src, dst, send_sem, recv_sem, to_d, to_m):
        copy = pltpu.make_async_remote_copy(
            src_ref=src,
            dst_ref=dst,
            send_sem=send_sem,
            recv_sem=recv_sem,
            device_id=(to_d, to_m),
            device_id_type=MESH,
        )
        copy.start()
        sends.append(copy)

    def arrived(ref, send_sem, recv_sem):
        pltpu.make_async_remote_copy(
            src_ref=ref,
            dst_ref=ref,
            send_sem=send_sem,
            recv_sem=recv_sem,
            device_id=(partner, m),
            device_id_type=MESH,
        ).wait_recv()

    def came(k):
        return wrap(m - k, members)

    def goes(k):
        return wrap(m + k, members)

    def slot(p, member, device, half=None):
        length = piece if half is None else piece // 2
        start = member * block + device * piece + (0 if half is None else half * length)
        return weights.at[p, pl.ds(pl.multiple_of(start, length), length), :]

    def tower_slot(device, half=None):
        length = depth if half is None else depth // 2
        start = device * depth + (0 if half is None else half * length)
        return tower_all.at[pl.ds(pl.multiple_of(start, length), length), :]

    def source(p):
        return (down, up)[p % 2].at[p // 2]

    barrier = pltpu.get_barrier_semaphore()
    for k in range(1, members):
        pl.semaphore_signal(barrier, inc=1, device_id=(d, goes(k)), device_id_type=MESH)
    for i in range(1, groups):
        pl.semaphore_signal(barrier, inc=1, device_id=(wrap(d + i, groups), m), device_id_type=MESH)

    ids_copy = load(ids_hbm, ids)
    table_copy = load(table.at[0], table_half)
    weight_copies = []
    for p in range(pieces):
        here = pl.ds(pl.multiple_of(m * block, block), block)
        weight_copies.append(load(source(p), weights.at[p, here, :]))
    bias_copy = load(bias, biases.at[m])
    order_copy = load(order_hbm, order)
    tower_copy = load(tower, tower_slot(d))
    tower_bias_copy = load(tower_bias_hbm, tower_bias)

    def spread(p):
        for k in range(1, members):
            here = slot(p, came(k), d)
            arrived(here, z_send.at[p, k], z_recv.at[p, k])
            send(here, here, plane_send.at[p, k, 0], plane_recv.at[p, k, 0], chip_x * 2 + c, m)
            send(here, here, plane_send.at[p, k, 1], plane_recv.at[p, k, 1], chip_y * 2 + c, m)
            send(here, here, plane_send.at[p, k, 2], plane_recv.at[p, k, 2], partner, m)

    def relay(p):
        for k in range(1, members):
            for j in range(2):
                chip = chips[j]
                here = slot(p, came(k), chip * 2 + c)
                arrived(here, plane_send.at[p, k, j], plane_recv.at[p, k, j])
                half = slot(p, came(k), chip * 2 + c, j)
                send(
                    half,
                    half,
                    diag_send.at[p, k, j],
                    diag_recv.at[p, k, j],
                    chips[1 - j] * 2 + c,
                    m,
                )
                send(here, here, pair_send.at[p, k, j], pair_recv.at[p, k, j], partner, m)

    def finish_diag(p, k):
        for j in range(2):
            half = slot(p, came(k), chip_z * 2 + c, j)
            arrived(half, diag_send.at[p, k, j], diag_recv.at[p, k, j])
        here = slot(p, came(k), chip_z * 2 + c)
        send(here, here, pair_send.at[p, k, 2], pair_recv.at[p, k, 2], partner, m)

    def diag(p):
        for k in range(1, members):
            finish_diag(p, k)

    def complete(p, k):
        if k == 0:
            weight_copies[p].wait()
            return
        here = slot(p, came(k), partner)
        arrived(here, plane_send.at[p, k, 2], plane_recv.at[p, k, 2])
        for j in range(3):
            here = slot(p, came(k), chips[j] * 2 + 1 - c)
            arrived(here, pair_send.at[p, k, j], pair_recv.at[p, k, j])

    def tower_spread():
        here = tower_slot(d)
        send(here, here, t_plane_send.at[0], t_plane_recv.at[0], chip_x * 2 + c, m)
        send(here, here, t_plane_send.at[1], t_plane_recv.at[1], chip_y * 2 + c, m)
        send(here, here, t_plane_send.at[2], t_plane_recv.at[2], partner, m)

    def tower_relay():
        for j in range(2):
            here = tower_slot(chips[j] * 2 + c)
            arrived(here, t_plane_send.at[j], t_plane_recv.at[j])
            half = tower_slot(chips[j] * 2 + c, j)
            send(half, half, t_diag_send.at[j], t_diag_recv.at[j], chips[1 - j] * 2 + c, m)
            send(here, here, t_pair_send.at[j], t_pair_recv.at[j], partner, m)

    def tower_diag():
        for j in range(2):
            half = tower_slot(chip_z * 2 + c, j)
            arrived(half, t_diag_send.at[j], t_diag_recv.at[j])
        here = tower_slot(chip_z * 2 + c)
        send(here, here, t_pair_send.at[2], t_pair_recv.at[2], partner, m)

    def tower_complete():
        arrived(tower_slot(partner), t_plane_send.at[2], t_plane_recv.at[2])
        for j in range(3):
            here = tower_slot(chips[j] * 2 + 1 - c)
            arrived(here, t_pair_send.at[j], t_pair_recv.at[j])

    step = 16 if rows % 16 == 0 else 8

    def pool(group):
        first = pl.multiple_of((group * members + m) * rows, rows)

        def some(index, carry):
            base = pl.multiple_of(index * step, step)
            for r in range(step):
                total = None
                for hot in range(hots):
                    at = ids[hot, first + base + r]
                    row = table_wide[pl.ds(at, 1), :]
                    total = row if total is None else total + row
                sums[pl.ds(base + r, 1), :] = total
            return carry

        lax.fori_loop(0, rows // step, some, 0)
        return sums[...].astype(jnp.bfloat16)

    def pool_out(i):
        outbox[i] = pool(wrap(d + i, groups))

    def pool_away(i):
        to = wrap(d + i, groups)
        send(outbox.at[i], pooled.at[d], pool_send.at[i], pool_recv.at[i], to, m)

    table_copy.wait()
    table_wide[...] = table_half[...].astype(jnp.float32)
    ids_copy.wait()
    early = 2
    for i in range(1, early + 1):
        pool_out(i)
    pl.semaphore_wait(barrier, members - 1 + groups - 1)

    for p in range(pieces):
        for k in range(1, members):
            own = pl.ds(pl.multiple_of(d * piece, piece), piece)
            send(
                source(p).at[own, :],
                slot(p, m, d),
                z_send.at[p, k],
                z_recv.at[p, k],
                d,
                goes(k),
            )
        if p == 0:
            for k in range(1, members):
                send(bias, biases.at[m], bias_send.at[k], bias_recv.at[k], d, goes(k))
    for i in range(1, groups):
        if i > early:
            pool_out(i)
        pool_away(i)
    pooled[d] = pool(d)

    spread(0)
    spread(1)
    relay(0)
    order_copy.wait()
    for i in range(1, groups):
        arrived(pooled.at[wrap(d - i, groups)], pool_send.at[i], pool_recv.at[i])
    per_block = block // embed
    for b in range(members):
        features = [pooled[order[b * per_block + f]] for f in range(per_block)]
        embedded[b] = jnp.concatenate(features, axis=1)
    bias_copy.wait()
    for k in range(1, members):
        arrived(biases.at[came(k)], bias_send.at[k], bias_recv.at[k])
    for p in range(2, pieces):
        spread(p)
        relay(p - 1)
        diag(p - 2)
    relay(pieces - 1)
    tower_copy.wait()
    tower_spread()
    diag(pieces - 2)

    def matching(p, b):
        return weights[p, pl.ds(pl.multiple_of(b * block, block), block), :]

    for layer in range(layers):
        p = 2 * layer
        last = layer == layers - 1
        state = embedded if layer == 0 else crossed
        projected = None
        for k in range(members):
            complete(p, k)
            b = came(k)
            term = jnp.dot(state[b], matching(p, b), preferred_element_type=jnp.float32)
            projected = term if projected is None else projected + term
        projected = projected.astype(jnp.bfloat16)
        for k in range(members):
            if last and k + 1 < members:
                finish_diag(p + 1, k + 1)
            complete(p + 1, k)
            b = came(k)
            lifted = lax.dot_general(
                projected,
                matching(p + 1, b),
                (((1,), (1,)), ((), ())),
                preferred_element_type=jnp.float32,
            )
            wide = embedded[b].astype(jnp.float32)
            value = wide * (lifted + biases[b, layer : layer + 1, :]) + state[b].astype(jnp.float32)
            value = value.astype(jnp.bfloat16)
            if not last:
                crossed[b] = value
                continue
            crossed_all[m, b] = value
            for to in range(1, members):
                send(
                    crossed_all.at[m, b],
                    crossed_all.at[m, b],
                    cross_send.at[k, to],
                    cross_recv.at[k, to],
                    d,
                    goes(to),
                )

    tower_relay()
    tower_diag()
    tower_bias_copy.wait()
    tower_complete()

    def finish(member):
        value = None
        for b in range(members):
            part = jnp.dot(
                crossed_all[member, b],
                tower_all[b * block : (b + 1) * block, :],
                preferred_element_type=jnp.float32,
            )
            value = part if value is None else value + part
        value = jnp.maximum(value + tower_bias[...], 0.0).astype(jnp.bfloat16)
        out[pl.ds(pl.multiple_of(member * rows, rows), rows), :] = value

    finish(m)
    for to in sorted(range(1, members), key=lambda k: min(k, members - k)):
        sender = came(to)
        for k in range(members):
            here = crossed_all.at[sender, wrap(sender - k, members)]
            arrived(here, cross_send.at[k, to], cross_recv.at[k, to])
        finish(sender)
    for copy in sends:
        copy.wait_send()


def fused_body(
    feature_ids,
    tables,
    table_of_feature,
    cross_down,
    cross_up,
    cross_bias,
    tower_weight,
    tower_bias,
):
    groups = lax.axis_size("dp")
    members = lax.axis_size("mp")
    _, batch_size, hot_count = feature_ids.shape
    rows = batch_size // (groups * members)
    _, vocab, embed = tables.shape
    layers, block, rank = cross_down.shape
    depth, units = tower_weight.shape
    width = block * members
    pieces = 2 * layers
    dma = pltpu.SemaphoreType.DMA
    anywhere = pl.BlockSpec(memory_space=pl.ANY)
    vmem = pl.BlockSpec(memory_space=pltpu.VMEM)
    return pl.pallas_call(
        functools.partial(kernel, groups, members),
        out_shape=jax.ShapeDtypeStruct((rows * members, units), jnp.bfloat16),
        in_specs=[anywhere] * 8,
        out_specs=vmem,
        scratch_shapes=[
            pltpu.SMEM((hot_count, batch_size), jnp.int32),
            pltpu.SMEM(table_of_feature.shape, jnp.int32),
            pltpu.VMEM((vocab, embed), jnp.bfloat16),
            pltpu.VMEM((vocab, embed), jnp.float32),
            pltpu.VMEM((rows, embed), jnp.float32),
            pltpu.VMEM((groups, rows, embed), jnp.bfloat16),
            pltpu.VMEM((groups, rows, embed), jnp.bfloat16),
            pltpu.VMEM((members, rows, block), jnp.bfloat16),
            pltpu.VMEM((members, rows, block), jnp.bfloat16),
            pltpu.VMEM((pieces, width, rank), jnp.bfloat16),
            pltpu.VMEM((members, layers, block), jnp.float32),
            pltpu.VMEM((width, units), jnp.bfloat16),
            pltpu.VMEM((1, units), jnp.float32),
            pltpu.VMEM((members, members, rows, block), jnp.bfloat16),
            dma((6 + pieces,)),
            dma((pieces, members)),
            dma((pieces, members)),
            dma((pieces, members, 3)),
            dma((pieces, members, 3)),
            dma((pieces, members, 2)),
            dma((pieces, members, 2)),
            dma((pieces, members, 3)),
            dma((pieces, members, 3)),
            dma((members,)),
            dma((members,)),
            dma((3,)),
            dma((3,)),
            dma((2,)),
            dma((2,)),
            dma((3,)),
            dma((3,)),
            dma((groups,)),
            dma((groups,)),
            dma((members, members)),
            dma((members, members)),
        ],
        compiler_params=pltpu.CompilerParams(
            collective_id=0, has_side_effects=True, vmem_limit_bytes=VMEM_BYTES
        ),
    )(
        feature_ids[0].T,
        table_of_feature,
        tables,
        cross_down,
        cross_up,
        cross_bias,
        tower_weight,
        tower_bias.reshape(1, -1),
    )


def body(
    feature_ids,
    tables,
    table_of_feature,
    cross_down,
    cross_up,
    cross_bias,
    tower_weight,
    tower_bias,
):
    groups = lax.axis_size("dp")
    members = lax.axis_size("mp")
    held = 2 * members * (cross_down.size + cross_up.size) + 2 * groups * tower_weight.size
    fits = held <= KERNEL_BYTES and groups == 2 * CHIPS and tables.shape[0] == 1
    chosen = fused_body if fits else plain_body
    return chosen(
        feature_ids,
        tables,
        table_of_feature,
        cross_down,
        cross_up,
        cross_bias,
        tower_weight,
        tower_bias,
    )


def solution(mesh):
    return jax.shard_map(
        body,
        mesh=mesh,
        in_specs=(
            P("dp", None, None),
            P("dp", None, None),
            P(),
            P(None, "mp", None),
            P(None, "mp", None),
            P(None, "mp"),
            P("dp", "mp"),
            P("mp"),
        ),
        out_specs=P("dp", "mp"),
        check_vma=False,
    )
```

time: 53.4 us -> 47.1 us (0.88)
  local copies, waits for them, and re-layouts: 5.79 us -> 1.67 us
  Pallas kernels: 47 us -> 45.2 us
    unnamed x15 -> x1, local copies, waits for them, and re-layouts: 4.62 us -> 1.67 us
    pallas_call x1, Pallas kernels: 47 us -> 45.2 us  [fused_body(): pl.pallas_call(functools.partial(kernel, groups, members), out_shape=jax....]
    reshape x2 -> x0, local copies, waits for them, and re-layouts: 1.07 us -> none  [the longest x1 0.99 us: fused_body(): shaped = feature_ids[0].T.reshape(hot_count, groups, members, rows)]
where the time goes in v2:
time: 47.1 us; the launch traced here: 46.9 us
  Pallas kernels  45.2 us (96%)
  local copies, waits for them, and re-layouts  1.67 us (4%)
    pallas_call x1, Pallas kernels, fused_body(): pl.pallas_call(functools.partial(kernel, groups, members), out_shape=jax....  45.2 us
    unnamed x1, local copies, waits for them, and re-layouts  1.67 us

profile of v2, /device:TPU:0, one launch (start us, length us, event | category | flops | bytes accessed | tf_op | source)
XLA Modules:
  0.0 46.9 jit_solution(3301972380299131140)
XLA Ops:
  0.0 45.2 %shard_map.82 = bf16[256,512]{1,0:T(8,128)(2,1)} custom-call(s32[8,2048]{1,0:T(8,128)} %bitcast.4, s32[8]{0:T(128)} %order_hbm.1, bf16[1,4096,128]{2,1,0:T(8,128)(2,1)} %table.1, bf16[2,256,512]{2,1,0:T(8,128)(2,1)} %down.1, bf16[2,256,512]{2,1,0:T(8,128)(2,1)} %up.1, f32[2,256]{1,0:T(2,128)} %bias.1, bf16[128,512]{1,0:T(8,128)(2,1)} %tower.1, f32[1,512]{1,0:T(1,128)} %bitcast.5), custom_call_target="tpu_custom_call" | custom-call | tf_op jit(solution)/shard_map/pallas_call | solution.py:446
  45.2 1.7 %copy.10 = bf16[256,512]{1,0:T(8,128)(2,1)} copy(bf16[256,512]{1,0:T(8,128)(2,1)} %shard_map.82) | data formatting | bytes 524288

commit v3 on v2

--- a/solution.py
+++ b/solution.py
@@ -445,7 +445,7 @@
     vmem = pl.BlockSpec(memory_space=pltpu.VMEM)
     return pl.pallas_call(
         functools.partial(kernel, groups, members),
-        out_shape=jax.ShapeDtypeStruct((rows * members, units), jnp.bfloat16),
+        out_shape=pltpu.VMEM((rows * members, units), jnp.bfloat16),
         in_specs=[anywhere] * 8,
         out_specs=vmem,
         scratch_shapes=[

time: 47.1 us -> 45.4 us (0.964)
  local copies, waits for them, and re-layouts: 1.67 us -> 0.71 us
  Pallas kernels: 45.2 us -> 44.5 us
    unnamed x1, local copies, waits for them, and re-layouts: 1.67 us -> 0.71 us
    pallas_call x1, Pallas kernels: 45.2 us -> 44.5 us  [fused_body(): pl.pallas_call(functools.partial(kernel, groups, members), out_shape=pltp...]
where the time goes in v3:
time: 45.4 us; the launch traced here: 45.2 us
  Pallas kernels  44.5 us (98%)
  local copies, waits for them, and re-layouts  0.71 us (2%)
    pallas_call x1, Pallas kernels, fused_body(): pl.pallas_call(functools.partial(kernel, groups, members), out_shape=pltp...  44.5 us

profile of v3, /device:TPU:0, one launch (start us, length us, event | category | flops | bytes accessed | tf_op | source)
XLA Modules:
  0.0 45.2 jit_solution(7961983364393673256)
XLA Ops:
  0.0 44.5 %shard_map.82 = bf16[256,512]{1,0:T(8,128)(2,1)S(1)} custom-call(s32[8,2048]{1,0:T(8,128)} %bitcast.4, s32[8]{0:T(128)} %order_hbm.1, bf16[1,4096,128]{2,1,0:T(8,128)(2,1)} %table.1, bf16[2,256,512]{2,1,0:T(8,128)(2,1)} %down.1, bf16[2,256,512]{2,1,0:T(8,128)(2,1)} %up.1, f32[2,256]{1,0:T(2,128)} %bias.1, bf16[128,512]{1,0:T(8,128)(2,1)} %tower.1, ...), custom_call_target="tpu_custom_call" | custom-call | tf_op jit(solution)/shard_map/pallas_call | solution.py:446
  44.5 0.7 %copy.10 = bf16[256,512]{1,0:T(8,128)(2,1)} copy(bf16[256,512]{1,0:T(8,128)(2,1)S(1)} %shard_map.82) | data formatting | bytes 524288
